TPU v7x, 32 devices: a whole 2x2x4 slice. The times are simulated.
32 devices in a mesh: pr: 8 (over y, x, core), pc: 4 (over z).
Axes of the slice: x: 2, y: 2, z: 4, core: 2. Of those that a mesh axis runs over, the one named last changes fastest.
Arguments:
- pair_array: bfloat16 [256, 256, 128], P('pr', 'pc'), may hold values from -6 to 6
- left_weight: bfloat16 [128, 128], replicated, may hold values from -0.5 to 0.5
- right_weight: bfloat16 [128, 128], replicated, may hold values from -0.5 to 0.5
- left_gate: bfloat16 [128, 128], replicated, may hold values from -0.5 to 0.5
- right_gate: bfloat16 [128, 128], replicated, may hold values from -0.5 to 0.5
- mid_gain: float32 [128], replicated, may hold values from 0.25 to 1.75
- out_weight: bfloat16 [128, 128], replicated, may hold values from -0.5 to 0.5
- out_gate: bfloat16 [128, 128], replicated, may hold values from -0.5 to 0.5
Outputs:
- pair_update: bfloat16 [256, 256, 128], P('pr', 'pc')
All inputs are finite; a program needn't handle non-finite values.
Results may differ from a plain program's by a relative error of at most 0.012.
Values may be sent and summed in bfloat16 or wider, within the bound.
A program may use at most 128 MiB of HBM per device.

v0:
```python
import jax
import jax.numpy as jnp
from jax import lax
from jax.sharding import PartitionSpec as P


def unit_channels(values, channel_gain):
    centred = values - jnp.mean(values, axis=-1, keepdims=True)
    return (
        centred
        * lax.rsqrt(jnp.mean(centred * centred, axis=-1, keepdims=True) + 1e-05)
        * channel_gain
    )


def make_factors(pair_in, left_weight, right_weight, left_gate, right_gate):
    left = jnp.einsum("ijc,cd->ijd", pair_in, left_weight, preferred_element_type=jnp.float32)
    left = left * jax.nn.sigmoid(
        jnp.einsum("ijc,cd->ijd", pair_in, left_gate, preferred_element_type=jnp.float32)
    )
    right = jnp.einsum("ijc,cd->ijd", pair_in, right_weight, preferred_element_type=jnp.float32)
    right = right * jax.nn.sigmoid(
        jnp.einsum("ijc,cd->ijd", pair_in, right_gate, preferred_element_type=jnp.float32)
    )
    return (pair_in, left.astype(jnp.bfloat16), right.astype(jnp.bfloat16))


def to_pair(mixed, ready, mid_gain, out_weight, out_gate):
    scaled = unit_channels(mixed.astype(jnp.float32), mid_gain).astype(jnp.bfloat16)
    scaled = lax.optimization_barrier(scaled)
    gate = jax.nn.sigmoid(
        jnp.einsum("ijc,cd->ijd", ready, out_gate, preferred_element_type=jnp.float32)
    )
    return (
        jnp.einsum("ijd,dc->ijc", scaled, out_weight, preferred_element_type=jnp.float32) * gate
    ).astype(jnp.bfloat16)


def on_device(
    pair_array, left_weight, right_weight, left_gate, right_gate, mid_gain, out_weight, out_gate
):
    ready, left, right = make_factors(pair_array, left_weight, right_weight, left_gate, right_gate)
    count = pair_array.shape[0] * lax.axis_size("pr")
    left_lines, right_lines = (
        lax.all_to_all(left, "pr", split_axis=2, concat_axis=0, tiled=True),
        lax.all_to_all(right, "pr", split_axis=2, concat_axis=0, tiled=True),
    )
    strip = jnp.einsum(
        "kid,kjd->ijd",
        lax.all_gather(left_lines, "pc", axis=1, tiled=True),
        right_lines,
        preferred_element_type=jnp.float32,
    )
    strip = (strip * count ** (-0.5)).astype(jnp.bfloat16)
    mixed = lax.all_to_all(strip, "pr", split_axis=0, concat_axis=2, tiled=True)
    return to_pair(mixed, ready, mid_gain, out_weight, out_gate)


def solution(mesh):
    return jax.shard_map(
        on_device,
        mesh=mesh,
        in_specs=(P("pr", "pc", None), P(), P(), P(), P(), P(), P(), P()),
        out_specs=P("pr", "pc", None),
        check_vma=False,
    )
```

profile of v0, /device:TPU:0, one launch (start us, length us, event | category | flops | bytes accessed | tf_op | source)
XLA Modules:
  0.0 104.0 jit_solution(1541400130074911763)
XLA Ops:
  6.5 1.0 copy-done
  7.6 1.0 fusion.24
  8.6 1.2 %fusion.14 = bf16[32,64,128]{2,1,0:T(8,128)(2,1)S(1)} fusion(f32[32,64,128]{2,1,0:T(8,128)S(1)} %fusion.24, bf16[32,64,128]{2,1,0:T(8,128)(2,1)S(1)} %copy-done, bf16[128,128]{1,0:T(8,128)(2,1)} %param.11), kind=kOutput, calls=%fused_computation.22 | convolution fusion | flops 68419584 | bytes 2129920 | tf_op jit(solution)/shard_map/ijc,cd->ijd/dot_general | solution.py:19
  9.8 1.6 %copy.25 = bf16[32,64,128]{1,0,2:T(8,128)(2,1)S(1)} copy(bf16[32,64,128]{2,1,0:T(8,128)(2,1)S(1)} %fusion.14) | data formatting | bytes 1048576 | tf_op jit(solution)/shard_map/convert_element_type | solution.py:25
  11.4 0.7 reshape.28
  12.2 14.7 %all_to_all.45 = bf16[8,2,16384]{2,1,0:T(2,128)(2,1)S(1)} all-to-all(bf16[8,2,16384]{2,1,0:T(2,128)(2,1)S(1)} %reshape.28), channel_id=1, replica_groups=mesh['pr'=8,'pc'=4] {'pr'}, dimensions={0} | all-to-all | bytes 1048576 | tf_op jit(solution)/shard_map/all_to_all | solution.py:45
  26.8 0.7 reshape.29
  27.5 0.4 copy.27
  28.0 1.6 %copy.28 = bf16[256,64,16]{0,1,2:T(8,128)(2,1)} copy(bf16[256,64,16]{1,2,0:T(8,128)(2,1)S(1)} %bitcast.66) | data formatting | bytes 1048576 | tf_op jit(solution)/shard_map/all_to_all | solution.py:45
  29.6 0.3 fusion.27
  29.9 0.4 fusion.15
  30.4 1.6 %copy.22 = bf16[32,64,128]{1,0,2:T(8,128)(2,1)S(1)} copy(bf16[32,64,128]{2,1,0:T(8,128)(2,1)S(1)} %fusion.15) | data formatting | bytes 1048576 | tf_op jit(solution)/shard_map/convert_element_type | solution.py:25
  32.0 0.7 reshape.30
  32.7 12.1 %all_to_all.46 = bf16[8,2,16384]{2,1,0:T(2,128)(2,1)S(1)} all-to-all(bf16[8,2,16384]{2,1,0:T(2,128)(2,1)S(1)} %reshape.30), channel_id=1, replica_groups=mesh['pr'=8,'pc'=4] {'pr'}, dimensions={0} | all-to-all | bytes 1048576 | tf_op jit(solution)/shard_map/all_to_all | solution.py:46
  44.8 0.7 reshape.31
  45.5 0.4 copy.24
  45.9 28.9 %all-gather.2.cloned.1.call-done = bf16[256,256,16]{0,1,2:T(8,128)(2,1)} async-done(((bf16[256,64,16]{0,1,2:T(8,128)(2,1)}), bf16[256,256,16]{0,1,2:T(8,128)(2,1)}) %all-gather.2.cloned.1.call-update) | async-done | bytes 2097168 | tf_op jit(solution)/shard_map/all_gather | solution.py:50
  74.8 2.4 %fusion.18 = bf16[256,64,16]{0,1,2:T(8,128)(2,1)S(1)} fusion(bf16[256,256,16]{0,1,2:T(8,128)(2,1)} %all-gather.2.cloned.1.call-done, bf16[256,64,16]{1,2,0:T(8,128)(2,1)S(1)} %bitcast.61), kind=kOutput, calls=%fused_computation.26 | convolution fusion | flops 134742016 | bytes 3145728 | tf_op jit(solution)/shard_map/kid,kjd->ijd/dot_general | solution.py:48
  77.2 1.0 copy.30
  78.1 1.5 %reshape.32 = bf16[8,2,16384]{2,1,0:T(2,128)(2,1)} reshape(bf16[256,16,64]{2,1,0:T(8,128)(2,1)S(1)} %bitcast.64) | data formatting | bytes 1048576
  79.6 3.7 %all-to-all-start.2 = ((bf16[8,2,16384]{2,1,0:T(2,128)(2,1)}), bf16[8,2,16384]{2,1,0:T(2,128)(2,1)S(1)}, u32[]{:S(2)}, u32[]{:S(2)}) async-start(bf16[8,2,16384]{2,1,0:T(2,128)(2,1)} %reshape.32), calls=%async_computation.2 | async-start | bytes 1048576 | tf_op jit(solution)/shard_map/all_to_all | solution.py:55
  83.3 0.4 fusion.13
  83.8 9.3 %all-to-all-done.2 = bf16[8,2,16384]{2,1,0:T(2,128)(2,1)S(1)} async-done(((bf16[8,2,16384]{2,1,0:T(2,128)(2,1)}), bf16[8,2,16384]{2,1,0:T(2,128)(2,1)S(1)}, u32[]{:S(2)}, u32[]{:S(2)}) %all-to-all-start.2) | async-done | bytes 524320 | tf_op jit(solution)/shard_map/all_to_all | solution.py:55
  93.0 0.7 reshape.33
  93.7 0.2 convert_bitcast_fusion
  93.9 0.2 fusion.19
  94.1 0.4 multiply_reduce_fusion
  94.5 0.3 copy.31
  94.8 0.4 copy-done.3
  95.2 0.5 fusion.2
  95.6 0.3 copy-done.2
  95.9 1.3 %fusion.17 = bf16[32,64,128]{2,1,0:T(8,128)(2,1)} fusion(f32[32,64,128]{2,1,0:T(8,128)S(1)} %fusion.13, bf16[32,64,128]{1,2,0:T(8,128)(2,1)S(1)} %fusion.2, bf16[128,128]{1,0:T(8,128)(2,1)S(1)} %copy-done.2), kind=kOutput, calls=%fused_computation.25 | convolution fusion | flops 67633152 | bytes 2129920 | tf_op jit(solution)/shard_map/ijd,dc->ijc/dot_general | solution.py:35
  (13 shorter events, 0.1 us)
Async XLA Ops:
  6.5 1.0 %copy-start = (bf16[32,64,128]{2,1,0:T(8,128)(2,1)S(1)}, bf16[32,64,128]{2,1,0:T(8,128)(2,1)}, u32[]{:S(2)}) copy-start(bf16[32,64,128]{2,1,0:T(8,128)(2,1)} %param.8) | copy-start | bytes 1572868
  6.5 68.3 %all-gather.2.cloned.1.call-start = ((), (), s32[]{:S(2)}) async-start(), calls=%async_computation.3 | async-start | bytes 2621440 | tf_op jit(solution)/shard_map/all_gather | solution.py:50
  27.5 2.1 %copy-start.1 = (bf16[128,128]{1,0:T(8,128)(2,1)S(1)}, bf16[128,128]{1,0:T(8,128)(2,1)}, u32[]{:S(2)}) copy-start(bf16[128,128]{1,0:T(8,128)(2,1)} %param.10) | copy-start | bytes 98308
  27.9 2.0 %copy-start.4 = (bf16[128,128]{1,0:T(8,128)(2,1)S(1)}, bf16[128,128]{1,0:T(8,128)(2,1)}, u32[]{:S(2)}) copy-start(bf16[128,128]{1,0:T(8,128)(2,1)} %param.12) | copy-start | bytes 98308
  77.2 6.2 %copy-start.5 = (bf16[128,128]{1,0:T(8,128)(2,1)S(1)}, bf16[128,128]{1,0:T(8,128)(2,1)}, u32[]{:S(2)}) copy-start(bf16[128,128]{1,0:T(8,128)(2,1)} %param.15) | copy-start | bytes 98308
  79.6 13.4 %all-to-all-start.2 = ((bf16[8,2,16384]{2,1,0:T(2,128)(2,1)}), bf16[8,2,16384]{2,1,0:T(2,128)(2,1)S(1)}, u32[]{:S(2)}, u32[]{:S(2)}) async-start(bf16[8,2,16384]{2,1,0:T(2,128)(2,1)} %reshape.32), calls=%async_computation.2 | async-start | bytes 1048576 | tf_op jit(solution)/shard_map/all_to_all | solution.py:55
  94.5 0.7 copy-start.3
  95.2 0.8 copy-start.2
Sparse Core Ops, SparseCore 0:
  29.7 45.0 all-gather.1
where the time goes:
time: 105 us; the launch traced here: 104 us
  waiting for transfers between devices  38.2 us (36%)
  blocking collectives  26.8 us (26%)
  between operations  13.6 us (13%)
  local copies, waits for them, and re-layouts  13.5 us (13%)
  matrix products  6.96 us (7%)
  starting transfers between devices  3.68 us (4%)
  other arithmetic  1.27 us (1%)
    all_gather x1, waiting for transfers between devices, on_device(): lax.all_gather(left_lines, 'pc', axis=1, tiled=True)  28.9 us
    all_to_all x1, blocking collectives, on_device(): lax.all_to_all(left, 'pr', split_axis=2, concat_axis=0, tiled=True)  14.7 us
    all_to_all x1, blocking collectives, on_device(): lax.all_to_all(right, 'pr', split_axis=2, concat_axis=0, tiled=True)  12.1 us
    all_to_all x1, waiting for transfers between devices, on_device(): mixed = lax.all_to_all(strip, 'pr', split_axis=0, concat_axis=2, tiled=True)  9.25 us
    unnamed x18, local copies, waits for them, and re-layouts  6.59 us
    all_to_all x1, starting transfers between devices, on_device(): mixed = lax.all_to_all(strip, 'pr', split_axis=0, concat_axis=2, tiled=True)  3.67 us
    convert_element_type x2, local copies, waits for them, and re-layouts, make_factors(): return (pair_in, left.astype(jnp.bfloat16), right.astype(jnp.bfloat16))  3.24 us
    dot_general x1, matrix products, on_device(): jnp.einsum('kid,kjd->ijd', lax.all_gather(left_lines, 'pc', axis=1, tiled...  2.35 us
  transfers between devices with their start and end apart: 2, of which 2 were waited for; matrix products, arithmetic and copies ran while one was open for 4% of the time, Pallas kernels for 0%

commit v1 on v0

--- a/solution.py
+++ b/solution.py
@@ -45,12 +45,19 @@
         lax.all_to_all(left, "pr", split_axis=2, concat_axis=0, tiled=True),
         lax.all_to_all(right, "pr", split_axis=2, concat_axis=0, tiled=True),
     )
-    strip = jnp.einsum(
-        "kid,kjd->ijd",
-        lax.all_gather(left_lines, "pc", axis=1, tiled=True),
-        right_lines,
-        preferred_element_type=jnp.float32,
-    )
+    size, index, rows = (lax.axis_size("pc"), lax.axis_index("pc"), left_lines.shape[1])
+    ahead = [(i, (i + 1) % size) for i in range(size)]
+    current, out = (left_lines, None)
+    for step in range(size):
+        source = (index - step) % size
+        upcoming = lax.ppermute(current, "pc", ahead) if step < size - 1 else None
+        made = jnp.einsum("kid,kjd->ijd", current, right_lines, preferred_element_type=jnp.float32)
+        length = made.shape[0]
+        if out is None:
+            out = jnp.zeros((*made.shape[:0], size * length, *made.shape[0 + 1 :]), made.dtype)
+        out = lax.dynamic_update_slice_in_dim(out, made, source * length, axis=0)
+        current = upcoming
+    strip = out
     strip = (strip * count ** (-0.5)).astype(jnp.bfloat16)
     mixed = lax.all_to_all(strip, "pr", split_axis=0, concat_axis=2, tiled=True)
     return to_pair(mixed, ready, mid_gain, out_weight, out_gate)

time: 105 us -> 93.3 us (0.89)
  blocking collectives: 26.8 us -> 0 us
  starting transfers between devices: 3.68 us -> 19.4 us
  between operations: 13.6 us -> 0.24 us
  local copies, waits for them, and re-layouts: 13.5 us -> 25.5 us
  waiting for transfers between devices: 38.2 us -> 30.1 us
  matrix products: 6.96 us -> 14.5 us
  other arithmetic: 1.27 us -> 2.42 us
    all_gather x1 -> x0, waiting for transfers between devices: 28.9 us -> none  [on_device(): lax.all_gather(left_lines, 'pc', axis=1, tiled=True)]
    all_to_all x2 -> x0, blocking collectives: 26.8 us -> none  [the longest x1 14.7 us: on_device(): lax.all_to_all(left, 'pr', split_axis=2, concat_axis=0, tiled=True)]
    all_to_all x0 -> x2, waiting for transfers between devices: none -> 14.6 us  [the longest x1 8.46 us: on_device(): lax.all_to_all(left, 'pr', split_axis=2, concat_axis=0, tiled=True)]
    all_to_all x0 -> x2, starting transfers between devices: none -> 8.68 us  [the longest x1 5.18 us: on_device(): lax.all_to_all(left, 'pr', split_axis=2, concat_axis=0, tiled=True)]
    transpose x0 -> x4, local copies, waits for them, and re-layouts: none -> 6.54 us  [on_device(): jnp.einsum('kid,kjd->ijd', current, right_lines, preferred_element_type=j...]
    ppermute x0 -> x3, waiting for transfers between devices: none -> 6.2 us  [on_device(): upcoming = lax.ppermute(current, 'pc', ahead) if step < size - 1 else None]
    dot_general x1 -> x4, matrix products: 2.35 us -> 7.66 us  [on_device(): jnp.einsum('kid,kjd->ijd', current, right_lines, preferred_element_type=j...]
    all_to_all x1, starting transfers between devices: 3.67 us -> 8.61 us  [on_device(): mixed = lax.all_to_all(strip, 'pr', split_axis=0, concat_axis=2, tiled=True)]
  transfers between devices with their start and end apart: 2 -> 6, of which waited for: 2 -> 6; matrix products, arithmetic and copies ran while one was open for 4% -> 23% of each run, Pallas kernels for 0% -> 0%
where the time goes in v1:
time: 93.3 us; the launch traced here: 92.1 us
  waiting for transfers between devices  30.1 us (32%)
  local copies, waits for them, and re-layouts  25.5 us (27%)
  starting transfers between devices  19.4 us (21%)
  matrix products  14.5 us (16%)
  other arithmetic  2.42 us (3%)
    unnamed x22, local copies, waits for them, and re-layouts  10.6 us
    all_to_all x1, waiting for transfers between devices, on_device(): mixed = lax.all_to_all(strip, 'pr', split_axis=0, concat_axis=2, tiled=True)  9.27 us
    all_to_all x1, starting transfers between devices, on_device(): mixed = lax.all_to_all(strip, 'pr', split_axis=0, concat_axis=2, tiled=True)  8.61 us
    all_to_all x1, waiting for transfers between devices, on_device(): lax.all_to_all(left, 'pr', split_axis=2, concat_axis=0, tiled=True)  8.46 us
    dot_general x4, matrix products, on_device(): jnp.einsum('kid,kjd->ijd', current, right_lines, preferred_element_type=j...  7.66 us
    transpose x4, local copies, waits for them, and re-layouts, on_device(): jnp.einsum('kid,kjd->ijd', current, right_lines, preferred_element_type=j...  6.54 us
    ppermute x3, waiting for transfers between devices, on_device(): upcoming = lax.ppermute(current, 'pc', ahead) if step < size - 1 else None  6.2 us
    all_to_all x1, waiting for transfers between devices, on_device(): lax.all_to_all(right, 'pr', split_axis=2, concat_axis=0, tiled=True)  6.15 us
  transfers between devices with their start and end apart: 6, of which 6 were waited for; matrix products, arithmetic and copies ran while one was open for 23% of the time, Pallas kernels for 0%

profile of v1, /device:TPU:0, one launch (start us, length us, event | category | flops | bytes accessed | tf_op | source)
XLA Modules:
  0.0 92.1 jit_solution(16892351249505732541)
XLA Ops:
  0.0 1.0 %copy-done = bf16[32,64,128]{2,1,0:T(8,128)(2,1)S(1)} copy-done((bf16[32,64,128]{2,1,0:T(8,128)(2,1)S(1)}, bf16[32,64,128]{2,1,0:T(8,128)(2,1)}, u32[]{:S(2)}) %copy-start) | copy-done | bytes 524312
  1.0 1.0 %fusion.21 = f32[32,64,128]{2,1,0:T(8,128)S(1)} fusion(bf16[32,64,128]{2,1,0:T(8,128)(2,1)S(1)} %copy-done, bf16[128,128]{1,0:T(8,128)(2,1)} %param.9), kind=kOutput, calls=%fused_computation.33 | convolution fusion | flops 67108864 | bytes 1605632 | tf_op jit(solution)/shard_map/ijc,cd->ijd/dot_general | solution.py:17
  2.1 1.2 %fusion.14 = bf16[32,64,128]{2,1,0:T(8,128)(2,1)S(1)} fusion(f32[32,64,128]{2,1,0:T(8,128)S(1)} %fusion.21, bf16[32,64,128]{2,1,0:T(8,128)(2,1)S(1)} %copy-done, bf16[128,128]{1,0:T(8,128)(2,1)} %param.11), kind=kOutput, calls=%fused_computation.22 | convolution fusion | flops 68419584 | bytes 2129920 | tf_op jit(solution)/shard_map/ijc,cd->ijd/dot_general | solution.py:19
  3.3 1.6 %copy.30 = bf16[32,64,128]{1,0,2:T(8,128)(2,1)S(1)} copy(bf16[32,64,128]{2,1,0:T(8,128)(2,1)S(1)} %fusion.14) | data formatting | bytes 1048576 | tf_op jit(solution)/shard_map/convert_element_type | solution.py:25
  4.9 1.5 %reshape.30 = bf16[8,2,16384]{2,1,0:T(2,128)(2,1)} reshape(bf16[128,32,64]{2,1,0:T(8,128)(2,1)S(1)} %bitcast.75) | data formatting | bytes 1048576
  6.4 5.2 %all-to-all-start.1 = ((bf16[8,2,16384]{2,1,0:T(2,128)(2,1)}), bf16[8,2,16384]{2,1,0:T(2,128)(2,1)S(1)}, u32[]{:S(2)}, u32[]{:S(2)}) async-start(bf16[8,2,16384]{2,1,0:T(2,128)(2,1)} %reshape.30), calls=%async_computation.1 | async-start | bytes 1048576 | tf_op jit(solution)/shard_map/all_to_all | solution.py:45
  11.6 1.2 %fusion.24 = f32[32,64,128]{2,1,0:T(8,128)} fusion(bf16[32,64,128]{2,1,0:T(8,128)(2,1)S(1)} %copy-done, bf16[128,128]{1,0:T(8,128)(2,1)S(1)} %copy-done.3), kind=kOutput, calls=%fused_computation.36 | convolution fusion | flops 67108864 | bytes 1605632 | tf_op jit(solution)/shard_map/ijc,cd->ijd/dot_general | solution.py:21
  12.9 8.5 %all-to-all-done.1 = bf16[8,2,16384]{2,1,0:T(2,128)(2,1)S(1)} async-done(((bf16[8,2,16384]{2,1,0:T(2,128)(2,1)}), bf16[8,2,16384]{2,1,0:T(2,128)(2,1)S(1)}, u32[]{:S(2)}, u32[]{:S(2)}) %all-to-all-start.1) | async-done | bytes 524320 | tf_op jit(solution)/shard_map/all_to_all | solution.py:45
  23.3 1.6 %collective-permute-start = (bf16[256,64,16]{0,1,2:T(8,128)(2,1)S(1)}, bf16[256,64,16]{0,1,2:T(8,128)(2,1)}, u32[]{:S(2)}, u32[]{:S(2)}) collective-permute-start(bf16[256,64,16]{0,1,2:T(8,128)(2,1)S(1)} %copy.34), channel_id=1, source_target_pairs={{0,1},{1,2},{2,3},{3,0},{4,5},{5,6},{6,7},{7,4},{8,9},{9,10},{10,1... | collective-permute-start | bytes 1572872 | tf_op jit(solution)/shard_map/ppermute | solution.py:53
  24.9 1.6 %fusion.15 = bf16[32,64,128]{2,1,0:T(8,128)(2,1)S(1)} fusion(f32[32,64,128]{2,1,0:T(8,128)} %fusion.24, bf16[32,64,128]{2,1,0:T(8,128)(2,1)S(1)} %copy-done, bf16[128,128]{1,0:T(8,128)(2,1)S(1)} %copy-done.6), kind=kOutput, calls=%fused_computation.23 | convolution fusion | flops 68419584 | bytes 2129920 | tf_op jit(solution)/shard_map/ijc,cd->ijd/dot_general | solution.py:23
  26.6 1.6 %copy.27 = bf16[32,64,128]{1,0,2:T(8,128)(2,1)S(1)} copy(bf16[32,64,128]{2,1,0:T(8,128)(2,1)S(1)} %fusion.15) | data formatting | bytes 1048576 | tf_op jit(solution)/shard_map/convert_element_type | solution.py:25
  28.2 1.5 %reshape.28 = bf16[8,2,16384]{2,1,0:T(2,128)(2,1)} reshape(bf16[128,32,64]{2,1,0:T(8,128)(2,1)S(1)} %bitcast.76) | data formatting | bytes 1048576
  29.7 3.5 %all-to-all-start = ((bf16[8,2,16384]{2,1,0:T(2,128)(2,1)}), bf16[8,2,16384]{2,1,0:T(2,128)(2,1)S(1)}, u32[]{:S(2)}, u32[]{:S(2)}) async-start(bf16[8,2,16384]{2,1,0:T(2,128)(2,1)} %reshape.28), calls=%async_computation | async-start | bytes 1048576 | tf_op jit(solution)/shard_map/all_to_all | solution.py:46
  33.2 3.5 %collective-permute-done = bf16[256,64,16]{0,1,2:T(8,128)(2,1)} collective-permute-done((bf16[256,64,16]{0,1,2:T(8,128)(2,1)S(1)}, bf16[256,64,16]{0,1,2:T(8,128)(2,1)}, u32[]{:S(2)}, u32[]{:S(2)}) %collective-permute-start) | collective-permute-done | bytes 524320 | tf_op jit(solution)/shard_map/ppermute | solution.py:53
  36.7 6.1 %all-to-all-done = bf16[8,2,16384]{2,1,0:T(2,128)(2,1)S(1)} async-done(((bf16[8,2,16384]{2,1,0:T(2,128)(2,1)}), bf16[8,2,16384]{2,1,0:T(2,128)(2,1)S(1)}, u32[]{:S(2)}, u32[]{:S(2)}) %all-to-all-start) | async-done | bytes 524320 | tf_op jit(solution)/shard_map/all_to_all | solution.py:46
  44.8 1.3 %convolution_bitcast_fusion.3 = f32[64,64,16]{0,1,2:T(8,128)S(1)} fusion(bf16[256,64,16]{0,1,2:T(8,128)(2,1)S(1)} %copy.33, bf16[256,64,16]{0,1,2:T(8,128)(2,1)} %copy-done.1), kind=kOutput, calls=%fused_computation.28 | convolution fusion | flops 33554432 | bytes 1310720 | tf_op jit(solution)/shard_map/kid,kjd->ijd/dot_general | solution.py:54
  46.1 1.0 %copy.35 = f32[64,64,16]{1,2,0:T(8,128)} copy(f32[64,64,16]{0,1,2:T(8,128)S(1)} %convolution_bitcast_fusion.3) | data formatting | bytes 524288 | tf_op jit(solution)/shard_map/kid,kjd->ijd/transpose | solution.py:54
  48.2 1.3 %collective-permute-done.1 = bf16[256,64,16]{0,1,2:T(8,128)(2,1)} collective-permute-done((bf16[256,64,16]{0,1,2:T(8,128)(2,1)}, bf16[256,64,16]{0,1,2:T(8,128)(2,1)}, u32[]{:S(2)}, u32[]{:S(2)}) %collective-permute-start.1) | collective-permute-done | bytes 524320 | tf_op jit(solution)/shard_map/ppermute | solution.py:53
  50.0 2.1 %convolution_bitcast_fusion.2 = f32[64,64,16]{0,1,2:T(8,128)} fusion(bf16[256,64,16]{0,1,2:T(8,128)(2,1)S(1)} %copy.33, bf16[256,64,16]{0,1,2:T(8,128)(2,1)} %collective-permute-done), kind=kOutput, calls=%fused_computation.27 | convolution fusion | flops 33554432 | bytes 1310720 | tf_op jit(solution)/shard_map/kid,kjd->ijd/dot_general | solution.py:54
  52.2 2.1 %copy.38 = f32[64,64,16]{1,2,0:T(8,128)} copy(f32[64,64,16]{0,1,2:T(8,128)} %convolution_bitcast_fusion.2) | data formatting | bytes 524288 | tf_op jit(solution)/shard_map/kid,kjd->ijd/transpose | solution.py:54
  54.3 1.1 %constant_dynamic-update-slice_fusion.2 = f32[256,64,16]{1,2,0:T(8,128)S(1)} fusion(f32[256,64,16]{1,2,0:T(8,128)S(1)} %constant_dynamic-update-slice_fusion.3, f32[64,64,16]{1,2,0:T(8,128)} %copy.38, s32[]{:T(128)S(6)} %select_n.34), kind=kLoop, calls=%fused_computation.42 | loop fusion | bytes 786436 | tf_op jit(solution)/shard_map/dynamic_update_slice | solution.py:58
  55.3 2.1 %convolution_bitcast_fusion.1 = f32[64,64,16]{0,1,2:T(8,128)} fusion(bf16[256,64,16]{0,1,2:T(8,128)(2,1)S(1)} %copy.33, bf16[256,64,16]{0,1,2:T(8,128)(2,1)} %collective-permute-done.1), kind=kOutput, calls=%fused_computation.26 | convolution fusion | flops 33554432 | bytes 1310720 | tf_op jit(solution)/shard_map/kid,kjd->ijd/dot_general | solution.py:54
  57.4 2.1 %copy.40 = f32[64,64,16]{1,2,0:T(8,128)} copy(f32[64,64,16]{0,1,2:T(8,128)} %convolution_bitcast_fusion.1) | data formatting | bytes 524288 | tf_op jit(solution)/shard_map/kid,kjd->ijd/transpose | solution.py:54
  59.5 1.1 %constant_dynamic-update-slice_fusion.1 = f32[256,64,16]{1,2,0:T(8,128)S(1)} fusion(f32[256,64,16]{1,2,0:T(8,128)S(1)} %constant_dynamic-update-slice_fusion.2, f32[64,64,16]{1,2,0:T(8,128)} %copy.40, s32[]{:T(128)S(6)} %select_n.36), kind=kLoop, calls=%fused_computation.41 | loop fusion | bytes 786436 | tf_op jit(solution)/shard_map/dynamic_update_slice | solution.py:58
  60.6 1.4 %collective-permute-done.2 = bf16[256,64,16]{0,1,2:T(8,128)(2,1)} collective-permute-done((bf16[256,64,16]{0,1,2:T(8,128)(2,1)}, bf16[256,64,16]{0,1,2:T(8,128)(2,1)}, u32[]{:S(2)}, u32[]{:S(2)}) %collective-permute-start.2) | collective-permute-done | bytes 524320 | tf_op jit(solution)/shard_map/ppermute | solution.py:53
  62.0 2.1 %convolution_bitcast_fusion = f32[64,64,16]{0,1,2:T(8,128)} fusion(bf16[256,64,16]{0,1,2:T(8,128)(2,1)S(1)} %copy.33, bf16[256,64,16]{0,1,2:T(8,128)(2,1)} %collective-permute-done.2), kind=kOutput, calls=%fused_computation.25 | convolution fusion | flops 33554432 | bytes 1310720 | tf_op jit(solution)/shard_map/kid,kjd->ijd/dot_general | solution.py:54
  64.1 1.3 %copy.42 = f32[64,64,16]{1,2,0:T(8,128)S(1)} copy(f32[64,64,16]{0,1,2:T(8,128)} %convolution_bitcast_fusion) | data formatting | bytes 524288 | tf_op jit(solution)/shard_map/kid,kjd->ijd/transpose | solution.py:54
  65.5 1.2 %fusion.26 = bf16[256,16,64]{2,1,0:T(8,128)(2,1)} fusion(f32[256,64,16]{1,2,0:T(8,128)S(1)} %constant_dynamic-update-slice_fusion), kind=kLoop, calls=%fused_computation.44 | loop fusion | flops 524288 | bytes 1572864
  66.6 3.0 %reshape.32 = bf16[8,2,16384]{2,1,0:T(2,128)(2,1)} reshape(bf16[256,16,64]{2,1,0:T(8,128)(2,1)} %fusion.26) | data formatting | bytes 1048576
  69.6 8.6 %all-to-all-start.2 = ((bf16[8,2,16384]{2,1,0:T(2,128)(2,1)}), bf16[8,2,16384]{2,1,0:T(2,128)(2,1)S(1)}, u32[]{:S(2)}, u32[]{:S(2)}) async-start(bf16[8,2,16384]{2,1,0:T(2,128)(2,1)} %reshape.32), calls=%async_computation.2 | async-start | bytes 1048576 | tf_op jit(solution)/shard_map/all_to_all | solution.py:62
  78.7 9.3 %all-to-all-done.2 = bf16[8,2,16384]{2,1,0:T(2,128)(2,1)S(1)} async-done(((bf16[8,2,16384]{2,1,0:T(2,128)(2,1)}), bf16[8,2,16384]{2,1,0:T(2,128)(2,1)S(1)}, u32[]{:S(2)}, u32[]{:S(2)}) %all-to-all-start.2) | async-done | bytes 524320 | tf_op jit(solution)/shard_map/all_to_all | solution.py:62
  90.9 1.3 %fusion.16 = bf16[32,64,128]{2,1,0:T(8,128)(2,1)} fusion(f32[32,64,128]{2,1,0:T(8,128)S(1)} %fusion.13, bf16[32,64,128]{1,2,0:T(8,128)(2,1)S(1)} %fusion.2, bf16[128,128]{1,0:T(8,128)(2,1)S(1)} %copy-done.4), kind=kOutput, calls=%fused_computation.24 | convolution fusion | flops 67633152 | bytes 2129920 | tf_op jit(solution)/shard_map/ijd,dc->ijc/dot_general | solution.py:35
  (35 shorter events, 8.7 us)
Async XLA Ops:
  0.0 1.0 %copy-start = (bf16[32,64,128]{2,1,0:T(8,128)(2,1)S(1)}, bf16[32,64,128]{2,1,0:T(8,128)(2,1)}, u32[]{:S(2)}) copy-start(bf16[32,64,128]{2,1,0:T(8,128)(2,1)} %param.8) | copy-start | bytes 1572868
  3.3 8.3 %copy-start.3 = (bf16[128,128]{1,0:T(8,128)(2,1)S(1)}, bf16[128,128]{1,0:T(8,128)(2,1)}, u32[]{:S(2)}) copy-start(bf16[128,128]{1,0:T(8,128)(2,1)} %param.10) | copy-start | bytes 98308
  6.4 14.9 %all-to-all-start.1 = ((bf16[8,2,16384]{2,1,0:T(2,128)(2,1)}), bf16[8,2,16384]{2,1,0:T(2,128)(2,1)S(1)}, u32[]{:S(2)}, u32[]{:S(2)}) async-start(bf16[8,2,16384]{2,1,0:T(2,128)(2,1)} %reshape.30), calls=%async_computation.1 | async-start | bytes 1048576 | tf_op jit(solution)/shard_map/all_to_all | solution.py:45
  22.0 2.9 %copy-start.6 = (bf16[128,128]{1,0:T(8,128)(2,1)S(1)}, bf16[128,128]{1,0:T(8,128)(2,1)}, u32[]{:S(2)}) copy-start(bf16[128,128]{1,0:T(8,128)(2,1)} %param.12) | copy-start | bytes 98308
  23.3 3.3 %copy-start.1 = (bf16[256,64,16]{0,1,2:T(8,128)(2,1)}, bf16[256,64,16]{0,1,2:T(8,128)(2,1)S(1)}, u32[]{:S(2)}) copy-start(bf16[256,64,16]{0,1,2:T(8,128)(2,1)S(1)} %copy.34) | copy-start | bytes 1572868
  23.3 13.4 %collective-permute-start = (bf16[256,64,16]{0,1,2:T(8,128)(2,1)S(1)}, bf16[256,64,16]{0,1,2:T(8,128)(2,1)}, u32[]{:S(2)}, u32[]{:S(2)}) collective-permute-start(bf16[256,64,16]{0,1,2:T(8,128)(2,1)S(1)} %copy.34), channel_id=1, source_target_pairs={{0,1},{1,2},{2,3},{3,0},{4,5},{5,6},{6,7},{7,4},{8,9},{9,10},{10,1... | collective-permute-start | bytes 1572872 | tf_op jit(solution)/shard_map/ppermute | solution.py:53
  29.7 13.2 %all-to-all-start = ((bf16[8,2,16384]{2,1,0:T(2,128)(2,1)}), bf16[8,2,16384]{2,1,0:T(2,128)(2,1)S(1)}, u32[]{:S(2)}, u32[]{:S(2)}) async-start(bf16[8,2,16384]{2,1,0:T(2,128)(2,1)} %reshape.28), calls=%async_computation | async-start | bytes 1048576 | tf_op jit(solution)/shard_map/all_to_all | solution.py:46
  36.7 12.9 %collective-permute-start.1 = (bf16[256,64,16]{0,1,2:T(8,128)(2,1)}, bf16[256,64,16]{0,1,2:T(8,128)(2,1)}, u32[]{:S(2)}, u32[]{:S(2)}) collective-permute-start(bf16[256,64,16]{0,1,2:T(8,128)(2,1)} %collective-permute-done), channel_id=1, source_target_pairs={{0,1},{1,2},{2,3},{3,0},{4,5},{5,6},{6,7},{7,4},{8,9},{9,10},{10,1... | collective-permute-start | bytes 1572872 | tf_op jit(solution)/shard_map/ppermute | solution.py:53
  47.1 1.0 %copy-start.2 = (f32[64,64,16]{1,2,0:T(8,128)S(1)}, f32[64,64,16]{1,2,0:T(8,128)}, u32[]{:S(2)}) copy-start(f32[64,64,16]{1,2,0:T(8,128)} %copy.35) | copy-start | bytes 786436
  49.6 12.4 %collective-permute-start.2 = (bf16[256,64,16]{0,1,2:T(8,128)(2,1)}, bf16[256,64,16]{0,1,2:T(8,128)(2,1)}, u32[]{:S(2)}, u32[]{:S(2)}) collective-permute-start(bf16[256,64,16]{0,1,2:T(8,128)(2,1)} %collective-permute-done.1), channel_id=1, source_target_pairs={{0,1},{1,2},{2,3},{3,0},{4,5},{5,6},{6,7},{7,4},{8,9},{9,10},{10,1... | collective-permute-start | bytes 1572872 | tf_op jit(solution)/shard_map/ppermute | solution.py:53
  66.6 11.6 %copy-start.7 = (bf16[128,128]{1,0:T(8,128)(2,1)S(1)}, bf16[128,128]{1,0:T(8,128)(2,1)}, u32[]{:S(2)}) copy-start(bf16[128,128]{1,0:T(8,128)(2,1)} %param.15) | copy-start | bytes 98308
  69.6 18.3 %all-to-all-start.2 = ((bf16[8,2,16384]{2,1,0:T(2,128)(2,1)}), bf16[8,2,16384]{2,1,0:T(2,128)(2,1)S(1)}, u32[]{:S(2)}, u32[]{:S(2)}) async-start(bf16[8,2,16384]{2,1,0:T(2,128)(2,1)} %reshape.32), calls=%async_computation.2 | async-start | bytes 1048576 | tf_op jit(solution)/shard_map/all_to_all | solution.py:62
  89.5 0.7 copy-start.5
  90.1 0.8 copy-start.4
